TPU v7x, 32 devices: a whole 2x2x4 slice. The times are simulated.
32 devices in a mesh: seq: 8 (over y, x, core), vocab: 4 (over z).
Axes of the slice: x: 2, y: 2, z: 4, core: 2. Of those that a mesh axis runs over, the one named last changes fastest.
Arguments:
- hidden: bfloat16 [960, 4096], P('seq'), may hold values from -32 to 32
- head_weight: bfloat16 [4096, 98304], P(None, ('seq', 'vocab')), may hold values from -0.84375 to 0.84375
- labels: int32 [960], P('seq'), may hold values from 0 to 98303
- lengths: int32 [8], replicated, may hold values from 1 to 120, 480 in all
- pair_map: int32 [8], replicated, may hold values from 0 to 7, each once
- ref_margin: float32 [4], replicated, may hold values from -240 to 240
Outputs:
- seq_logps: float32 [8], replicated
- pair_loss: float32 [4], replicated
- z_loss: float32 [], replicated
Inputs may be any that keep to these rules, and one draw needn't show every extreme that they name: The lengths sum to 480 and the longest is exactly 120. Each response appears once; pair p compares response pair_map[2p], chosen, with response pair_map[2p+1], rejected.
All inputs are finite; a program needn't handle non-finite values.
Results may differ from a plain program's by a relative error of at most 0.0003.
Values may be sent and summed in bfloat16 or wider, within the bound.
No kernel may reach another device: no remote copies, remote signals or barrier semaphores. Data moves between devices by JAX's collectives and lax.ppermute only.
A program may use at most 192 MiB of HBM per device.

v0:
```python
import jax
import jax.numpy as jnp
from jax import lax
from jax.sharding import PartitionSpec as P

pref_beta = 0.05
zloss_weight = 0.0001


def per_device(hidden, head_weight, labels, lengths, pair_map, ref_margin):
    vocab_devices = lax.axis_size("vocab")
    shard_rows = hidden.shape[0]
    columns = head_weight.shape[1]
    seq_total = lengths.shape[0]
    col_first = (lax.axis_index("seq") * vocab_devices + lax.axis_index("vocab")) * columns
    col_ids = col_first + jnp.arange(columns, dtype=jnp.int32)
    seq_ids = jnp.arange(seq_total, dtype=jnp.int32)
    logits = jnp.dot(
        lax.all_gather(hidden, "seq", axis=0, tiled=True),
        head_weight,
        preferred_element_type=jnp.float32,
    )
    local_max = jnp.max(logits, axis=1)
    local_sum = jnp.sum(jnp.exp(logits - local_max[:, None]), axis=1)
    picked = jnp.sum(
        jnp.where(
            lax.all_gather(labels, "seq", axis=0, tiled=True)[:, None] == col_ids[None, :],
            logits,
            0.0,
        ),
        axis=1,
    )
    fresh = (local_max, local_sum, picked)
    local_max, local_sum, picked = tuple((fresh_part for fresh_part in fresh))
    top_score = lax.pmax(local_max, ("seq", "vocab"))
    exp_total, label_logit = lax.psum(
        (local_sum * jnp.exp(local_max - top_score), picked), ("seq", "vocab")
    )
    log_norm = (top_score + jnp.log(exp_total)).reshape(seq_total, shard_rows)
    label_logit = label_logit.reshape(seq_total, shard_rows)
    live_mask = jnp.arange(shard_rows, dtype=jnp.int32)[None, :] < lengths[:, None]
    seq_logps = jnp.sum(jnp.where(live_mask, label_logit - log_norm, 0.0), axis=1)
    select = (pair_map[:, None] == seq_ids[None, :]).astype(jnp.float32)
    ordered = jnp.dot(select, seq_logps, precision=lax.Precision.HIGHEST).reshape(seq_total // 2, 2)
    pair_loss = jax.nn.softplus(-pref_beta * (ordered[:, 0] - ordered[:, 1] - ref_margin))
    live_count = jnp.sum(live_mask.astype(jnp.float32))
    z_loss = zloss_weight * jnp.sum(jnp.where(live_mask, log_norm * log_norm, 0.0)) / live_count
    return (seq_logps, pair_loss, z_loss)


def solution(mesh):
    placed = (P("seq", None), P(None, ("seq", "vocab")), P("seq"), P(), P(), P())
    return jax.shard_map(
        per_device, mesh=mesh, in_specs=placed, out_specs=(P(), P(), P()), check_vma=False
    )
```

profile of v0, /device:TPU:0, one launch (start us, length us, event | category | flops | bytes accessed | tf_op | source)
XLA Modules:
  0.0 195.6 jit_solution(578517166683249568)
XLA Ops:
  7.2 0.0 all-gather.2.cloned.1.call-start
  7.2 0.7 all-gather.2.cloned.1.call-update
  7.9 0.7 iota_compare_fusion
  8.6 0.1 lt.20
  8.7 0.7 eq.32
  9.5 1.2 dynamic-slice
  11.4 0.9 dynamic-update-slice
  12.2 9.5 %all-reduce = s32[960]{0:T(1024)S(1)} all-reduce(s32[960]{0:T(1024)S(1)} %dynamic-update-slice), channel_id=1, replica_groups=mesh['seq'=8,'vocab'=4] {'seq'}, use_global_device_ids=true, to_apply=%add | all-reduce | flops 960 | bytes 7680
  21.7 42.9 %all-gather.2.cloned.1.call-done = bf16[960,4096]{1,0:T(8,128)(2,1)} async-done(((bf16[120,4096]{1,0:T(8,128)(2,1)}), bf16[960,4096]{1,0:T(8,128)(2,1)}) %all-gather.2.cloned.1.call-update) | async-done | bytes 7864336 | tf_op jit(solution)/shard_map/all_gather | solution.py:19
  64.7 32.4 %fusion.7 = (f32[960]{0:T(1024)S(1)}, f32[960,3072]{1,0:T(8,128)}) fusion(bf16[960,4096]{1,0:T(8,128)(2,1)} %all-gather.2.cloned.1.call-done, bf16[4096,3072]{1,0:T(8,128)(2,1)} %param.7), kind=kOutput, calls=%fused_computation.18 | convolution fusion | flops 24162140160 | bytes 44830464 | tf_op jit(solution)/shard_map/dot_general | solution.py:18
  97.1 0.0 copy-start.1
  97.1 0.0 copy-start
  97.1 39.3 %pmax.7 = f32[960]{0:T(1024)S(1)} all-reduce(f32[960]{0:T(1024)S(1)} %get-tuple-element.11), channel_id=1, replica_groups=mesh['seq'=8,'vocab'=4] {'seq','vocab'}, use_global_device_ids=true, to_apply=%region_3.4 | all-reduce | flops 960 | bytes 7680 | tf_op jit(solution)/shard_map/pmax | solution.py:35
  136.4 6.4 %exponential_reduce_fusion = (f32[960]{0:T(1024)S(1)}, f32[960]{0:T(1024)S(1)}) fusion(f32[960,3072]{1,0:T(8,128)} %get-tuple-element.12, f32[960]{0:T(1024)S(1)} %get-tuple-element.11, s32[3072]{0:T(1024)S(1)} %iota_add_fusion, s32[960]{0:T(1024)S(1)} %all-reduce), kind=kLoop, calls=%fused_computation | loop fusion | flops 14743680 | bytes 11824128 | tf_op jit(solution)/shard_map/reduce_sum | solution.py:24
  142.8 41.1 %all-reduce.1 = (f32[960]{0:T(1024)S(1)}, f32[960]{0:T(1024)S(1)}) all-reduce(f32[960]{0:T(1024)S(1)} %get-tuple-element.4, f32[960]{0:T(1024)S(1)} %exponential_multiply_fusion), channel_id=1, replica_groups=mesh['seq'=8,'vocab'=4] {'seq','vocab'}, use_global_device_ids=true, to_apply=%region_1.0 | all-reduce | flops 1920 | bytes 15360 | tf_op jit(solution)/shard_map/psum | solution.py:36
  183.8 0.6 select_reduce_fusion.1
  184.5 0.1 sub.30
  184.5 0.0 copy-done.1
  184.5 0.7 convert_reduce_fusion
  185.3 0.0 copy-start.2
  185.3 0.3 fusion
  185.6 0.1 copy.9
  185.7 0.0 copy-done
  185.7 0.5 compare_select_fusion
  187.6 0.0 copy-done.2
  (3 shorter events, 0.0 us)
Async XLA Ops:
  7.2 57.5 %all-gather.2.cloned.1.call-start = ((), (), s32[]{:S(2)}) async-start(), calls=%async_computation | async-start | bytes 8847360 | tf_op jit(solution)/shard_map/all_gather | solution.py:19
  97.1 87.4 %copy-start.1 = (s32[8]{0:T(128)S(1)}, s32[8]{0:T(128)}, u32[]{:S(2)}) copy-start(s32[8]{0:T(128)} %param.9) | copy-start | bytes 100
  97.1 88.6 %copy-start = (f32[4]{0:T(128)S(1)}, f32[4]{0:T(128)}, u32[]{:S(2)}) copy-start(f32[4]{0:T(128)} %param.11) | copy-start | bytes 52
  185.3 2.3 %copy-start.2 = (f32[8]{0:T(128)}, f32[8]{0:T(128)S(1)}, u32[]{:S(2)}) copy-start(f32[8]{0:T(128)S(1)} %get-tuple-element.6) | copy-start | bytes 100
Sparse Core Ops, SparseCore 0:
  9.9 54.7 all-gather.1
where the time goes:
time: 196 us
  blocking collectives  89.8 us (46%)
  waiting for transfers between devices  43.6 us (22%)
  matrix products  32.7 us (17%)
  between operations  17.2 us (9%)
  other arithmetic  9.04 us (5%)
  local copies, waits for them, and re-layouts  3.11 us (2%)
    all_gather x1, waiting for transfers between devices, per_device(): lax.all_gather(hidden, 'seq', axis=0, tiled=True)  42.9 us
    psum x1, blocking collectives, per_device(): lax.psum((local_sum * jnp.exp(local_max - top_score), picked), ('seq', 'v...  41.1 us
    pmax x1, blocking collectives, per_device(): top_score = lax.pmax(local_max, ('seq', 'vocab'))  39.3 us
    dot_general x1, matrix products, per_device(): jnp.dot(lax.all_gather(hidden, 'seq', axis=0, tiled=True), head_weight, p...  32.4 us
    unnamed x1, blocking collectives  9.49 us
    reduce_sum x1, other arithmetic, per_device(): local_sum = jnp.sum(jnp.exp(logits - local_max[:, None]), axis=1)  6.39 us
  transfers between devices with their start and end apart: 1, of which 1 were waited for; matrix products, arithmetic and copies ran while one was open for 2% of the time, Pallas kernels for 0%

commit v1 on v0

--- a/solution.py
+++ b/solution.py
@@ -1,13 +1,268 @@
+import functools
+
 import jax
 import jax.numpy as jnp
 from jax import lax
+from jax.experimental import pallas as pl
+from jax.experimental.pallas import tpu as pltpu
 from jax.sharding import PartitionSpec as P
 
 pref_beta = 0.05
 zloss_weight = 0.0001
-
-
-def per_device(hidden, head_weight, labels, lengths, pair_map, ref_margin):
+LANES = 128
+STRIPE = 8
+NEG = -1e30
+
+
+def softplus(x):
+    return jnp.maximum(x, 0.0) + jnp.log1p(jnp.exp(-jnp.abs(x)))
+
+
+def head_kernel(metas, depth, block, first, lens_ref, w_in, prev_ref, *rest):
+    pieces = rest[: len(metas)]
+    if first:
+        slab_ref, w_ref = rest[len(metas) : len(metas) + 2]
+        scratch = rest[len(metas) + 2 :]
+    else:
+        slab_ref, w_ref = rest[len(metas)], w_in
+        scratch = rest[len(metas) + 1 :]
+    x_buf, logit_buf, m_buf, s_buf, p_buf, lab_buf, lse_col, pick_col, x_sem, w_sem = scratch
+    responses = lens_ref.shape[0]
+    rows_max = x_buf.shape[0]
+    columns = w_ref.shape[1]
+    steps = columns // block
+    me = lax.axis_index("seq")
+    col_first = (me * lax.axis_size("vocab") + lax.axis_index("vocab")) * columns
+
+    def w_copy(n):
+        cols = pl.ds(pl.multiple_of(n * block, block), block)
+        return pltpu.make_async_copy(w_in.at[:, cols], w_ref.at[:, cols], w_sem.at[n])
+
+    offs, counts, total = [], [], jnp.int32(0)
+    for rel, pos, rows in metas:
+        live = jnp.clip(lens_ref[me ^ rel] - pos, 0, rows)
+        offs.append(total)
+        counts.append(live)
+        total = total + (live + STRIPE - 1) // STRIPE
+
+    def x_copy(j, b):
+        src = pieces[j].at[pl.ds(pl.multiple_of(b * STRIPE, STRIPE), STRIPE), :]
+        dst = x_buf.at[pl.ds(pl.multiple_of((offs[j] + b) * STRIPE, STRIPE), STRIPE), :]
+        return pltpu.make_async_copy(src, dst, x_sem)
+
+    for j in range(len(metas)):
+        @pl.loop(0, (counts[j] + STRIPE - 1) // STRIPE)
+        def _(b):
+            x_copy(j, b).start()
+
+    if first:
+        for n in range(steps):
+            w_copy(n).start()
+        slab_ref[...] = jnp.zeros_like(slab_ref)
+    else:
+        slab_ref[...] = prev_ref[...]
+
+    @pl.loop(0, total)
+    def _(b):
+        x_copy(0, 0).wait()
+
+    def compute(rows):
+        dig = x_buf[0:rows, depth : depth + LANES].astype(jnp.float32)
+        lab = dig[:, 0:1] + 256.0 * dig[:, 1:2] + 65536.0 * dig[:, 2:3]
+        lane = lax.broadcasted_iota(jnp.int32, (rows, LANES), 1)
+        lab_buf[0:rows, :] = lab.astype(jnp.int32) - col_first - lane
+        m_buf[0:rows, :] = jnp.full((rows, LANES), NEG, jnp.float32)
+        s_buf[0:rows, :] = jnp.zeros((rows, LANES), jnp.float32)
+        p_buf[0:rows, :] = jnp.zeros((rows, LANES), jnp.float32)
+        logit_buf[1, 0:rows, :] = jnp.full((rows, block), NEG, jnp.float32)
+
+        def reduce(slot, base):
+            for r0 in range(0, rows, 16):
+                r = slice(r0, r0 + min(16, rows - r0))
+                groups = [logit_buf[slot, r, g : g + LANES] for g in range(0, block, LANES)]
+                m_old = m_buf[r, :]
+                m_new = m_old
+                for a in groups:
+                    m_new = jnp.maximum(m_new, a)
+                s = s_buf[r, :] * jnp.exp(m_old - m_new)
+                p, lr = p_buf[r, :], lab_buf[r, :]
+                for g, a in enumerate(groups):
+                    s = s + jnp.exp(a - m_new)
+                    p = p + jnp.where(lr == base + g * LANES, a, 0.0)
+                m_buf[r, :], s_buf[r, :], p_buf[r, :] = m_new, s, p
+
+        @pl.loop(0, steps)
+        def _(n):
+            if first:
+                w_copy(n).wait()
+            slot = n % 2
+            cols = pl.ds(pl.multiple_of(n * block, block), block)
+            logit_buf[slot, 0:rows, :] = jnp.dot(
+                x_buf[0:rows, 0:depth], w_ref[:, cols], preferred_element_type=jnp.float32
+            )
+            reduce(1 - slot, jnp.where(n == 0, 1 << 30, (n - 1) * block))
+
+        reduce((steps - 1) % 2, (steps - 1) * block)
+        m = m_buf[0:rows, :]
+        top = jnp.max(m, axis=1, keepdims=True)
+        total_exp = jnp.sum(s_buf[0:rows, :] * jnp.exp(m - top), axis=1, keepdims=True)
+        lse_col[0:rows, :] = jnp.broadcast_to(top + jnp.log(total_exp), (rows, LANES))
+        pick = jnp.sum(p_buf[0:rows, :], axis=1, keepdims=True)
+        pick_col[0:rows, :] = jnp.broadcast_to(pick, (rows, LANES))
+
+    sizes = sorted({r for r in (128, 192) if r < rows_max} | {rows_max})
+    below = 0
+    for size in sizes:
+        @pl.when((total * STRIPE > below) & (total * STRIPE <= size))
+        def _():
+            compute(size)
+
+        below = size
+    if first:
+        @pl.when(total == 0)
+        def _():
+            for n in range(steps):
+                w_copy(n).wait()
+
+    lane = lax.broadcasted_iota(jnp.int32, (1, LANES), 1)
+    for j, (rel, pos, rows) in enumerate(metas):
+        @pl.when(counts[j] > 0)
+        def _():
+            at = pl.ds(pl.multiple_of(offs[j] * STRIPE, STRIPE), LANES)
+            here = (lane >= pos) & (lane < pos + counts[j])
+            for base, col in ((0, lse_col), (responses, pick_col)):
+                line = col[at, :].T[0:1, :]
+                if pos:
+                    line = pltpu.roll(line, pos, 1)
+                out = pl.ds(base + (me ^ rel), 1)
+                slab_ref[out, :] = slab_ref[out, :] + jnp.where(here, line, 0.0)
+
+
+def head_call(metas, depth, block, lengths, w, prev, pieces, first):
+    responses = lengths.shape[0]
+    rows = sum(m[2] for m in metas)
+    columns = w.shape[1]
+    vmem, smem, any_ = (
+        pl.BlockSpec(memory_space=pltpu.VMEM),
+        pl.BlockSpec(memory_space=pltpu.SMEM),
+        pl.BlockSpec(memory_space=pl.ANY),
+    )
+    slab = jax.ShapeDtypeStruct((2 * responses, LANES), jnp.float32)
+    out_shape, out_specs = slab, vmem
+    if first:
+        out_shape, out_specs = (slab, pltpu.VMEM(w.shape, w.dtype)), (vmem, vmem)
+    row_buf = pltpu.VMEM((rows, LANES), jnp.float32)
+    col_buf = pltpu.VMEM((rows + LANES, LANES), jnp.float32)
+    return pl.pallas_call(
+        functools.partial(head_kernel, metas, depth, block, first),
+        out_shape=out_shape,
+        in_specs=[smem, any_ if first else vmem, vmem] + [any_] * len(pieces),
+        out_specs=out_specs,
+        scratch_shapes=[
+            pltpu.VMEM((rows, pieces[0].shape[1]), jnp.bfloat16),
+            pltpu.VMEM((2, rows, block), jnp.float32),
+            row_buf,
+            row_buf,
+            row_buf,
+            pltpu.VMEM((rows, LANES), jnp.int32),
+            col_buf,
+            col_buf,
+            pltpu.SemaphoreType.DMA,
+            pltpu.SemaphoreType.DMA((columns // block,)),
+        ],
+        compiler_params=pltpu.CompilerParams(vmem_limit_bytes=(12 if not first else 12) << 20),
+        cost_estimate=pl.CostEstimate(
+            flops=rows * depth * columns, bytes_accessed=4 << 20, transcendentals=0
+        ),
+        name="head_first" if first else "head_next",
+    )(lengths, w, prev, *pieces)
+
+
+def loss_kernel(slabs_ref, lens_ref, pairs_ref, margin_ref, logp_ref, loss_ref, z_ref):
+    responses = lens_ref.shape[0]
+    devices = slabs_ref.shape[0]
+    top = slabs_ref[0, 0:responses, :]
+    for d in range(1, devices):
+        top = jnp.maximum(top, slabs_ref[d, 0:responses, :])
+    total = jnp.zeros_like(top)
+    picked = jnp.zeros_like(top)
+    for d in range(devices):
+        total = total + jnp.exp(slabs_ref[d, 0:responses, :] - top)
+        picked = picked + slabs_ref[d, responses : 2 * responses, :]
+    log_norm = top + jnp.log(total)
+    row = lax.broadcasted_iota(jnp.int32, (responses, LANES), 0)
+    lane = lax.broadcasted_iota(jnp.int32, (responses, LANES), 1)
+    lens = jnp.zeros((responses, LANES), jnp.int32)
+    count = jnp.int32(0)
+    for s in range(responses):
+        lens = jnp.where(row == s, lens_ref[s], lens)
+        count = count + lens_ref[s]
+    live = lane < lens
+    logp = jnp.sum(jnp.where(live, picked - log_norm, 0.0), axis=1, keepdims=True)
+    logp = jnp.broadcast_to(logp, (responses, LANES))
+    square = jnp.where(live, log_norm * log_norm, 0.0)
+    square = jnp.sum(jnp.sum(square, axis=1, keepdims=True), axis=0, keepdims=True)
+    one = lax.broadcasted_iota(jnp.int32, (1, LANES), 1)
+    margin = jnp.zeros((1, LANES), jnp.float32)
+    for p in range(responses // 2):
+        sign = jnp.where(row == pairs_ref[2 * p], 1.0, 0.0) - jnp.where(row == pairs_ref[2 * p + 1], 1.0, 0.0)
+        diff = jnp.sum(sign * logp, axis=0, keepdims=True) - margin_ref[p]
+        margin = jnp.where(one == p, diff, margin)
+    line = jnp.sum(jnp.where(row == lane, logp, 0.0), axis=0, keepdims=True)
+    logp_ref[...] = line
+    loss_ref[...] = softplus(-pref_beta * margin)
+    z_ref[...] = jnp.broadcast_to(zloss_weight * square / count.astype(jnp.float32), (1, LANES))
+
+
+def loss_call(slabs, lengths, pair_map, ref_margin):
+    vmem, smem = pl.BlockSpec(memory_space=pltpu.VMEM), pl.BlockSpec(memory_space=pltpu.SMEM)
+    line = jax.ShapeDtypeStruct((1, LANES), jnp.float32)
+    logp, loss, z = pl.pallas_call(
+        loss_kernel,
+        out_shape=(line, line, line),
+        in_specs=[vmem, smem, smem, smem],
+        out_specs=(vmem, vmem, vmem),
+        name="losses",
+    )(slabs, lengths, pair_map, ref_margin)
+    return logp[0, : lengths.shape[0]], loss[0, : ref_margin.shape[0]], z[0, 0]
+
+
+def square_device(hidden, head_weight, labels, lengths, pair_map, ref_margin):
+    seq = lax.axis_size("seq")
+    rows, depth = hidden.shape
+    half = -(-rows // 32) * 16
+
+    def swap(v, bit):
+        return lax.ppermute(v, "seq", [(i, i ^ bit) for i in range(seq)])
+
+    digits = jnp.stack([labels & 255, (labels >> 8) & 255, labels >> 16], axis=1)
+    digits = jnp.pad(digits.astype(jnp.bfloat16), ((0, 0), (0, LANES - 3)))
+    top = jnp.concatenate([hidden[:half], digits[:half]], axis=1)
+    low = jnp.concatenate([hidden[half:], digits[half:]], axis=1)
+    x_top, y_top = swap(top, 2), swap(top, 4)
+    c_top, c_low = swap(top, 1), swap(low, 1)
+    x_low, y_low = swap(low, 2), swap(low, 4)
+    d_top, d_low = swap(x_top, 4), swap(y_low, 2)
+    h = rows - half
+    T, L = (0, half), (half, h)
+    block = 512 if head_weight.shape[1] % 512 == 0 else LANES
+    call = functools.partial(head_call, depth=depth, block=block, lengths=lengths)
+    zero = jnp.zeros((2 * lengths.shape[0], LANES), jnp.float32)
+    slab, w = call(
+        metas=((0, *T), (0, *L), (1, *T), (1, *L)), w=head_weight, prev=zero,
+        pieces=[top, low, c_top, c_low], first=True,
+    )
+    for a, b, at, bits in ((x_top, y_top, T, (2, 4)), (x_low, y_low, L, (2, 4)), (d_top, d_low, None, (6, 6))):
+        ats = (T, L) if at is None else (at, at)
+        metas = tuple((bit ^ c, *t) for c in (0, 1) for bit, t in zip(bits, ats))
+        slab = call(metas=metas, w=w, prev=slab, pieces=[a, b, swap(a, 1), swap(b, 1)], first=False)
+    both = ("seq", "vocab")
+    n = lax.axis_size(both)
+    slabs = lax.all_to_all(jnp.broadcast_to(slab[None], (n, *slab.shape)), both, 0, 0)
+    return loss_call(slabs, lengths, pair_map, ref_margin)
+
+
+def general_device(hidden, head_weight, labels, lengths, pair_map, ref_margin):
     vocab_devices = lax.axis_size("vocab")
     shard_rows = hidden.shape[0]
     columns = head_weight.shape[1]
@@ -22,16 +277,8 @@
     )
     local_max = jnp.max(logits, axis=1)
     local_sum = jnp.sum(jnp.exp(logits - local_max[:, None]), axis=1)
-    picked = jnp.sum(
-        jnp.where(
-            lax.all_gather(labels, "seq", axis=0, tiled=True)[:, None] == col_ids[None, :],
-            logits,
-            0.0,
-        ),
-        axis=1,
-    )
-    fresh = (local_max, local_sum, picked)
-    local_max, local_sum, picked = tuple((fresh_part for fresh_part in fresh))
+    all_labels = lax.all_gather(labels, "seq", axis=0, tiled=True)
+    picked = jnp.sum(jnp.where(all_labels[:, None] == col_ids[None, :], logits, 0.0), axis=1)
     top_score = lax.pmax(local_max, ("seq", "vocab"))
     exp_total, label_logit = lax.psum(
         (local_sum * jnp.exp(local_max - top_score), picked), ("seq", "vocab")
@@ -50,6 +297,8 @@
 
 def solution(mesh):
     placed = (P("seq", None), P(None, ("seq", "vocab")), P("seq"), P(), P(), P())
+    square = mesh.shape["seq"] == 8
     return jax.shard_map(
-        per_device, mesh=mesh, in_specs=placed, out_specs=(P(), P(), P()), check_vma=False
-    )
+        square_device if square else general_device,
+        mesh=mesh, in_specs=placed, out_specs=(P(), P(), P()), check_vma=False,
+    )

time: 196 us -> 99.3 us (0.51)
  blocking collectives: 89.8 us -> 15 us
  Pallas kernels: 0 us -> 41 us
  matrix products: 32.7 us -> 0 us
  between operations: 17.2 us -> 0.76 us
  waiting for transfers between devices: 43.6 us -> 28.4 us
  starting transfers between devices: 0.04 us -> 10.1 us
  other arithmetic: 9.04 us -> 0.8 us
    all_gather x1 -> x0, waiting for transfers between devices: 42.9 us -> none  [per_device(): lax.all_gather(hidden, 'seq', axis=0, tiled=True)]
    psum x1 -> x0, blocking collectives: 41.1 us -> none  [per_device(): lax.psum((local_sum * jnp.exp(local_max - top_score), picked), ('seq', 'v...]
    pallas_call x0 -> x5, Pallas kernels: none -> 41 us  [the longest x4 39.3 us: head_call(): pl.pallas_call(functools.partial(head_kernel, metas, depth, block, first)...]
    pmax x1 -> x0, blocking collectives: 39.3 us -> none  [per_device(): top_score = lax.pmax(local_max, ('seq', 'vocab'))]
    dot_general x2 -> x0, matrix products: 32.7 us -> none  [the longest x1 32.4 us: per_device(): jnp.dot(lax.all_gather(hidden, 'seq', axis=0, tiled=True), head_weight, p...]
    ppermute x0 -> x14, waiting for transfers between devices: none -> 28.4 us  [swap(): return lax.ppermute(v, 'seq', [(i, i ^ bit) for i in range(seq)])]
    all_to_all x0 -> x1, blocking collectives: none -> 15 us  [square_device(): lax.all_to_all(jnp.broadcast_to(slab[None], (n, *slab.shape)), both, 0, 0)]
    ppermute x0 -> x14, starting transfers between devices: none -> 10.1 us  [swap(): return lax.ppermute(v, 'seq', [(i, i ^ bit) for i in range(seq)])]
  transfers between devices with their start and end apart: 1 -> 14, of which waited for: 1 -> 4; matrix products, arithmetic and copies ran while one was open for 2% -> 0% of each run, Pallas kernels for 0% -> 32%
where the time goes in v1:
time: 99.3 us; the launch traced here: 98.8 us
  Pallas kernels  41 us (41%)
  waiting for transfers between devices  28.4 us (29%)
  blocking collectives  15 us (15%)
  starting transfers between devices  10.1 us (10%)
  local copies, waits for them, and re-layouts  2.68 us (3%)
    pallas_call x4, Pallas kernels, head_call(): pl.pallas_call(functools.partial(head_kernel, metas, depth, block, first)...  39.3 us
    ppermute x14, waiting for transfers between devices, swap(): return lax.ppermute(v, 'seq', [(i, i ^ bit) for i in range(seq)])  28.4 us
    all_to_all x1, blocking collectives, square_device(): lax.all_to_all(jnp.broadcast_to(slab[None], (n, *slab.shape)), both, 0, 0)  15 us
    ppermute x14, starting transfers between devices, swap(): return lax.ppermute(v, 'seq', [(i, i ^ bit) for i in range(seq)])  10.1 us
    squeeze x2, local copies, waits for them, and re-layouts, loss_call(): return (logp[0, :lengths.shape[0]], loss[0, :ref_margin.shape[0]], z[0, 0])  2.34 us
  transfers between devices with their start and end apart: 14, of which 4 were waited for; matrix products, arithmetic and copies ran while one was open for 0% of the time, Pallas kernels for 32%

profile of v1, /device:TPU:0, one launch (start us, length us, event | category | flops | bytes accessed | tf_op | source)
XLA Modules:
  0.0 98.8 jit_solution(11128907465639420763)
XLA Ops:
  0.6 0.0 slice-start
  0.6 0.7 convert_bitcast_fusion.2
  1.4 0.1 copy.12
  1.5 0.1 slice-done
  1.7 0.0 slice-start.1
  1.7 0.0 copy-start
  1.7 0.6 collective-permute-start.1
  2.3 2.6 %collective-permute-start.7 = (bf16[56,4224]{1,0:T(8,128)(2,1)S(1)}, bf16[56,4224]{1,0:T(8,128)(2,1)S(1)}, u32[]{:S(2)}, u32[]{:S(2)}) collective-permute-start(bf16[56,4224]{1,0:T(8,128)(2,1)S(1)} %pad_maximum_fusion.1.rest_1_), channel_id=1, source_target_pairs={{0,16},{4,20},{8,24},{12,28},{16,0},{20,4},{24,8},{28,12},{1,17},{... | collective-permute-start | bytes 1419272 | tf_op jit(solution)/shard_map/ppermute | solution.py:236
  4.9 0.0 slice-done.1
  4.9 1.6 %collective-permute-start.2 = (bf16[64,4224]{1,0:T(8,128)(2,1)S(1)}, bf16[64,4224]{1,0:T(8,128)(2,1)S(1)}, u32[]{:S(2)}, u32[]{:S(2)}) collective-permute-start(bf16[64,4224]{1,0:T(8,128)(2,1)S(1)} %pad_maximum_fusion.rest_0_), channel_id=1, source_target_pairs={{0,8},{4,12},{8,0},{12,4},{16,24},{20,28},{24,16},{28,20},{1,9},{5... | collective-permute-start | bytes 1622024 | tf_op jit(solution)/shard_map/ppermute | solution.py:236
  6.5 0.8 collective-permute-start.3
  7.3 0.5 collective-permute-start.6
  7.8 0.0 collective-permute-done.1.rest_3_
  7.8 0.0 collective-permute-start
  7.8 8.7 %collective-permute-done.7.rest_1_ = bf16[56,4224]{1,0:T(8,128)(2,1)S(1)} collective-permute-done((bf16[56,4224]{1,0:T(8,128)(2,1)S(1)}, bf16[56,4224]{1,0:T(8,128)(2,1)S(1)}, u32[]{:S(2)}, u32[]{:S(2)}) %collective-permute-start.7) | collective-permute-done | bytes 473120 | tf_op jit(solution)/shard_map/ppermute | solution.py:236
  16.5 2.0 %collective-permute-start.11 = (bf16[56,4224]{1,0:T(8,128)(2,1)S(1)}, bf16[56,4224]{1,0:T(8,128)(2,1)S(1)}, u32[]{:S(2)}, u32[]{:S(2)}) collective-permute-start(bf16[56,4224]{1,0:T(8,128)(2,1)S(1)} %collective-permute-done.7.rest_1_), channel_id=1, source_target_pairs={{0,8},{4,12},{8,0},{12,4},{16,24},{20,28},{24,16},{28,20},{1,9},{5... | collective-permute-start | bytes 1419272 | tf_op jit(solution)/shard_map/ppermute | solution.py:236
  18.5 1.6 %collective-permute-done.2.rest_0_ = bf16[64,4224]{1,0:T(8,128)(2,1)S(1)} collective-permute-done((bf16[64,4224]{1,0:T(8,128)(2,1)S(1)}, bf16[64,4224]{1,0:T(8,128)(2,1)S(1)}, u32[]{:S(2)}, u32[]{:S(2)}) %collective-permute-start.2) | collective-permute-done | bytes 540704 | tf_op jit(solution)/shard_map/ppermute | solution.py:236
  20.1 0.0 collective-permute-start.4
  20.1 10.1 %collective-permute-done.6.rest_0_ = bf16[56,4224]{1,0:T(8,128)(2,1)S(1)} collective-permute-done((bf16[56,4224]{1,0:T(8,128)(2,1)S(1)}, bf16[56,4224]{1,0:T(8,128)(2,1)S(1)}, u32[]{:S(2)}, u32[]{:S(2)}) %collective-permute-start.6) | collective-permute-done | bytes 473120 | tf_op jit(solution)/shard_map/ppermute | solution.py:236
  30.3 0.8 collective-permute-start.10
  31.1 0.0 collective-permute-done.3.rest_1_
  31.1 0.0 collective-permute-start.5
  31.1 0.0 collective-permute-done.rest_2_
  31.1 0.5 collective-permute-start.9
  31.6 8.0 %collective-permute-done.11.rest_1_ = bf16[56,4224]{1,0:T(8,128)(2,1)S(1)} collective-permute-done((bf16[56,4224]{1,0:T(8,128)(2,1)S(1)}, bf16[56,4224]{1,0:T(8,128)(2,1)S(1)}, u32[]{:S(2)}, u32[]{:S(2)}) %collective-permute-start.11) | collective-permute-done | bytes 473120 | tf_op jit(solution)/shard_map/ppermute | solution.py:236
  39.6 0.0 collective-permute-start.8
  39.6 0.0 copy-done
  39.6 10.7 %head_first.1 = (f32[16,128]{1,0:T(8,128)S(1)}, bf16[4096,3072]{1,0:T(8,128)(2,1)S(1)}) custom-call(s32[8]{0:T(128)S(1)} %copy-done, bf16[4096,3072]{1,0:T(8,128)(2,1)} %w_in.1, f32[16,128]{1,0:T(8,128)S(1)} %broadcast_in_dim.4.prev_ref, bf16[64,4224]{1,0:T(8,128)(2,1)S(1)} %pad_maximum_fusion.rest_0_, bf16[56,4224]{1,0:T(8,128)(2,1)S(1)} %pad_maximum_fusion.1.rest_1_, ...), custom_call_target="tpu_custom_call" | custom-call | flops 3019898880 | bytes 4194304 | tf_op jit(solution)/shard_map/head_first/pallas_call | solution.py:156
  50.3 0.0 collective-permute-done.4.rest_2_
  50.3 0.6 collective-permute-start.13
  50.9 0.0 collective-permute-done.10.rest_0_
  50.9 0.1 collective-permute-start.12
  51.0 0.0 collective-permute-done.5.rest_3_
  51.0 12.9 %head_next.3.prev_ref = f32[16,128]{1,0:T(8,128)S(1)} custom-call(s32[8]{0:T(128)S(1)} %copy-done, bf16[4096,3072]{1,0:T(8,128)(2,1)S(1)} %get-tuple-element.8.w_in, f32[16,128]{1,0:T(8,128)S(1)} %get-tuple-element.9.prev_ref, bf16[64,4224]{1,0:T(8,128)(2,1)S(1)} %collective-permute-done.2.rest_0_, bf16[64,4224]{1,0:T(8,128)(2,1)S(1)} %collective-permute-done.3.rest_1_, ...), custom_call_target="tpu_custom_call" | custom-call | flops 3221225472 | bytes 4194304 | tf_op jit(solution)/shard_map/head_next/pallas_call | solution.py:156
  63.9 0.0 collective-permute-done.9.rest_3_
  64.0 0.0 collective-permute-done.8.rest_2_
  64.0 7.9 %head_next.4.prev_ref = f32[16,128]{1,0:T(8,128)S(1)} custom-call(s32[8]{0:T(128)S(1)} %copy-done, bf16[4096,3072]{1,0:T(8,128)(2,1)S(1)} %get-tuple-element.8.w_in, f32[16,128]{1,0:T(8,128)S(1)} %head_next.3.prev_ref, bf16[56,4224]{1,0:T(8,128)(2,1)S(1)} %collective-permute-done.6.rest_0_, bf16[56,4224]{1,0:T(8,128)(2,1)S(1)} %collective-permute-done.7.rest_1_, ...), custom_call_target="tpu_custom_call" | custom-call | flops 2818572288 | bytes 4194304 | tf_op jit(solution)/shard_map/head_next/pallas_call | solution.py:156
  71.9 0.0 collective-permute-done.13.rest_3_
  71.9 0.0 collective-permute-done.12.rest_2_
  71.9 7.7 %head_next.5 = f32[16,128]{1,0:T(8,128)S(1)} custom-call(s32[8]{0:T(128)S(1)} %copy-done, bf16[4096,3072]{1,0:T(8,128)(2,1)S(1)} %get-tuple-element.8.w_in, f32[16,128]{1,0:T(8,128)S(1)} %head_next.4.prev_ref, bf16[64,4224]{1,0:T(8,128)(2,1)S(1)} %collective-permute-done.10.rest_0_, bf16[56,4224]{1,0:T(8,128)(2,1)S(1)} %collective-permute-done.11.rest_1_, ...), custom_call_target="tpu_custom_call" | custom-call | flops 3019898880 | bytes 4194304 | tf_op jit(solution)/shard_map/head_next/pallas_call | solution.py:156
  79.7 15.0 %all_to_all.5.slabs_ref = f32[32,16,128]{2,1,0:T(8,128)} all-to-all(f32[32,16,128]{2,1,0:T(8,128)S(1)} %broadcast_in_dim.10), channel_id=1, replica_groups=mesh['seq'=8,'vocab'=4] {'seq','vocab'}, dimensions={0} | all-to-all | bytes 524288 | tf_op jit(solution)/shard_map/all_to_all | solution.py:261
  94.7 1.7 %losses.1 = (f32[1,128]{1,0:T(1,128)}, f32[1,128]{1,0:T(1,128)}, f32[1,128]{1,0:T(1,128)}) custom-call(f32[32,16,128]{2,1,0:T(8,128)} %all_to_all.5.slabs_ref, s32[8]{0:T(128)} %lens_ref.9, s32[8]{0:T(128)} %pairs_ref.1, f32[4]{0:T(128)} %margin_ref.1), custom_call_target="tpu_custom_call" | custom-call | tf_op jit(solution)/shard_map/losses/pallas_call | solution.py:220
  96.4 1.2 %slice_bitcast_fusion = f32[4]{0:T(128)} fusion(f32[1,128]{1,0:T(1,128)} %get-tuple-element.11), kind=kLoop, calls=%fused_computation.5 | loop fusion | bytes 32 | tf_op jit(solution)/shard_map/squeeze | solution.py:227
  97.6 1.2 %slice_bitcast_fusion.1 = f32[8]{0:T(128)} fusion(f32[1,128]{1,0:T(1,128)} %get-tuple-element.10), kind=kLoop, calls=%fused_computation.6 | loop fusion | bytes 64 | tf_op jit(solution)/shard_map/squeeze | solution.py:227
  (7 shorter events, 0.1 us)
Async XLA Ops:
  0.6 1.0 %slice-start = ((bf16[120,4096]{1,0:T(8,128)(2,1)}), bf16[56,4096]{1,0:T(8,128)(2,1)S(1)}, s32[]{:S(2)}) async-start(bf16[120,4096]{1,0:T(8,128)(2,1)} %param.6), calls=%async_computation.1 | async-start | bytes 917504 | tf_op jit(solution)/shard_map/slice | solution.py:241
  1.7 3.2 %slice-start.1 = ((bf16[120,4096]{1,0:T(8,128)(2,1)}), bf16[64,4096]{1,0:T(8,128)(2,1)S(1)}, s32[]{:S(2)}) async-start(bf16[120,4096]{1,0:T(8,128)(2,1)} %param.6), calls=%async_computation.2 | async-start | bytes 1048576 | tf_op jit(solution)/shard_map/slice | solution.py:240
  1.7 37.9 %copy-start = (s32[8]{0:T(128)S(1)}, s32[8]{0:T(128)}, u32[]{:S(2)}) copy-start(s32[8]{0:T(128)} %lens_ref.9) | copy-start | bytes 100
  1.7 6.1 %collective-permute-start.1 = (bf16[56,4224]{1,0:T(8,128)(2,1)S(1)}, bf16[56,4224]{1,0:T(8,128)(2,1)S(1)}, u32[]{:S(2)}, u32[]{:S(2)}) collective-permute-start(bf16[56,4224]{1,0:T(8,128)(2,1)S(1)} %pad_maximum_fusion.1.rest_1_), channel_id=1, source_target_pairs={{0,4},{4,0},{8,12},{12,8},{16,20},{20,16},{24,28},{28,24},{1,5},{5... | collective-permute-start | bytes 1419272 | tf_op jit(solution)/shard_map/ppermute | solution.py:236
  2.3 14.3 %collective-permute-start.7 = (bf16[56,4224]{1,0:T(8,128)(2,1)S(1)}, bf16[56,4224]{1,0:T(8,128)(2,1)S(1)}, u32[]{:S(2)}, u32[]{:S(2)}) collective-permute-start(bf16[56,4224]{1,0:T(8,128)(2,1)S(1)} %pad_maximum_fusion.1.rest_1_), channel_id=1, source_target_pairs={{0,16},{4,20},{8,24},{12,28},{16,0},{20,4},{24,8},{28,12},{1,17},{... | collective-permute-start | bytes 1419272 | tf_op jit(solution)/shard_map/ppermute | solution.py:236
  4.9 15.2 %collective-permute-start.2 = (bf16[64,4224]{1,0:T(8,128)(2,1)S(1)}, bf16[64,4224]{1,0:T(8,128)(2,1)S(1)}, u32[]{:S(2)}, u32[]{:S(2)}) collective-permute-start(bf16[64,4224]{1,0:T(8,128)(2,1)S(1)} %pad_maximum_fusion.rest_0_), channel_id=1, source_target_pairs={{0,8},{4,12},{8,0},{12,4},{16,24},{20,28},{24,16},{28,20},{1,9},{5... | collective-permute-start | bytes 1622024 | tf_op jit(solution)/shard_map/ppermute | solution.py:236
  6.5 24.6 %collective-permute-start.3 = (bf16[64,4224]{1,0:T(8,128)(2,1)S(1)}, bf16[64,4224]{1,0:T(8,128)(2,1)S(1)}, u32[]{:S(2)}, u32[]{:S(2)}) collective-permute-start(bf16[64,4224]{1,0:T(8,128)(2,1)S(1)} %pad_maximum_fusion.rest_0_), channel_id=1, source_target_pairs={{0,16},{4,20},{8,24},{12,28},{16,0},{20,4},{24,8},{28,12},{1,17},{... | collective-permute-start | bytes 1622024 | tf_op jit(solution)/shard_map/ppermute | solution.py:236
  7.3 23.0 %collective-permute-start.6 = (bf16[56,4224]{1,0:T(8,128)(2,1)S(1)}, bf16[56,4224]{1,0:T(8,128)(2,1)S(1)}, u32[]{:S(2)}, u32[]{:S(2)}) collective-permute-start(bf16[56,4224]{1,0:T(8,128)(2,1)S(1)} %pad_maximum_fusion.1.rest_1_), channel_id=1, source_target_pairs={{0,8},{4,12},{8,0},{12,4},{16,24},{20,28},{24,16},{28,20},{1,9},{5... | collective-permute-start | bytes 1419272 | tf_op jit(solution)/shard_map/ppermute | solution.py:236
  7.8 23.3 %collective-permute-start = (bf16[64,4224]{1,0:T(8,128)(2,1)S(1)}, bf16[64,4224]{1,0:T(8,128)(2,1)S(1)}, u32[]{:S(2)}, u32[]{:S(2)}) collective-permute-start(bf16[64,4224]{1,0:T(8,128)(2,1)S(1)} %pad_maximum_fusion.rest_0_), channel_id=1, source_target_pairs={{0,4},{4,0},{8,12},{12,8},{16,20},{20,16},{24,28},{28,24},{1,5},{5... | collective-permute-start | bytes 1622024 | tf_op jit(solution)/shard_map/ppermute | solution.py:236
  16.5 23.1 %collective-permute-start.11 = (bf16[56,4224]{1,0:T(8,128)(2,1)S(1)}, bf16[56,4224]{1,0:T(8,128)(2,1)S(1)}, u32[]{:S(2)}, u32[]{:S(2)}) collective-permute-start(bf16[56,4224]{1,0:T(8,128)(2,1)S(1)} %collective-permute-done.7.rest_1_), channel_id=1, source_target_pairs={{0,8},{4,12},{8,0},{12,4},{16,24},{20,28},{24,16},{28,20},{1,9},{5... | collective-permute-start | bytes 1419272 | tf_op jit(solution)/shard_map/ppermute | solution.py:236
  20.1 30.2 %collective-permute-start.4 = (bf16[64,4224]{1,0:T(8,128)(2,1)S(1)}, bf16[64,4224]{1,0:T(8,128)(2,1)S(1)}, u32[]{:S(2)}, u32[]{:S(2)}) collective-permute-start(bf16[64,4224]{1,0:T(8,128)(2,1)S(1)} %collective-permute-done.2.rest_0_), channel_id=1, source_target_pairs={{0,4},{4,0},{8,12},{12,8},{16,20},{20,16},{24,28},{28,24},{1,5},{5... | collective-permute-start | bytes 1622024 | tf_op jit(solution)/shard_map/ppermute | solution.py:236
  30.3 20.6 %collective-permute-start.10 = (bf16[64,4224]{1,0:T(8,128)(2,1)S(1)}, bf16[64,4224]{1,0:T(8,128)(2,1)S(1)}, u32[]{:S(2)}, u32[]{:S(2)}) collective-permute-start(bf16[64,4224]{1,0:T(8,128)(2,1)S(1)} %collective-permute-done.2.rest_0_), channel_id=1, source_target_pairs={{0,16},{4,20},{8,24},{12,28},{16,0},{20,4},{24,8},{28,12},{1,17},{... | collective-permute-start | bytes 1622024 | tf_op jit(solution)/shard_map/ppermute | solution.py:236
  31.1 19.9 %collective-permute-start.5 = (bf16[64,4224]{1,0:T(8,128)(2,1)S(1)}, bf16[64,4224]{1,0:T(8,128)(2,1)S(1)}, u32[]{:S(2)}, u32[]{:S(2)}) collective-permute-start(bf16[64,4224]{1,0:T(8,128)(2,1)S(1)} %collective-permute-done.3.rest_1_), channel_id=1, source_target_pairs={{0,4},{4,0},{8,12},{12,8},{16,20},{20,16},{24,28},{28,24},{1,5},{5... | collective-permute-start | bytes 1622024 | tf_op jit(solution)/shard_map/ppermute | solution.py:236
  31.1 32.8 %collective-permute-start.9 = (bf16[56,4224]{1,0:T(8,128)(2,1)S(1)}, bf16[56,4224]{1,0:T(8,128)(2,1)S(1)}, u32[]{:S(2)}, u32[]{:S(2)}) collective-permute-start(bf16[56,4224]{1,0:T(8,128)(2,1)S(1)} %collective-permute-done.7.rest_1_), channel_id=1, source_target_pairs={{0,4},{4,0},{8,12},{12,8},{16,20},{20,16},{24,28},{28,24},{1,5},{5... | collective-permute-start | bytes 1419272 | tf_op jit(solution)/shard_map/ppermute | solution.py:236
  39.6 24.4 %collective-permute-start.8 = (bf16[56,4224]{1,0:T(8,128)(2,1)S(1)}, bf16[56,4224]{1,0:T(8,128)(2,1)S(1)}, u32[]{:S(2)}, u32[]{:S(2)}) collective-permute-start(bf16[56,4224]{1,0:T(8,128)(2,1)S(1)} %collective-permute-done.6.rest_0_), channel_id=1, source_target_pairs={{0,4},{4,0},{8,12},{12,8},{16,20},{20,16},{24,28},{28,24},{1,5},{5... | collective-permute-start | bytes 1419272 | tf_op jit(solution)/shard_map/ppermute | solution.py:236
  50.3 21.6 %collective-permute-start.13 = (bf16[56,4224]{1,0:T(8,128)(2,1)S(1)}, bf16[56,4224]{1,0:T(8,128)(2,1)S(1)}, u32[]{:S(2)}, u32[]{:S(2)}) collective-permute-start(bf16[56,4224]{1,0:T(8,128)(2,1)S(1)} %collective-permute-done.11.rest_1_), channel_id=1, source_target_pairs={{0,4},{4,0},{8,12},{12,8},{16,20},{20,16},{24,28},{28,24},{1,5},{5... | collective-permute-start | bytes 1419272 | tf_op jit(solution)/shard_map/ppermute | solution.py:236
  50.9 21.0 %collective-permute-start.12 = (bf16[64,4224]{1,0:T(8,128)(2,1)S(1)}, bf16[64,4224]{1,0:T(8,128)(2,1)S(1)}, u32[]{:S(2)}, u32[]{:S(2)}) collective-permute-start(bf16[64,4224]{1,0:T(8,128)(2,1)S(1)} %collective-permute-done.10.rest_0_), channel_id=1, source_target_pairs={{0,4},{4,0},{8,12},{12,8},{16,20},{20,16},{24,28},{28,24},{1,5},{5... | collective-permute-start | bytes 1622024 | tf_op jit(solution)/shard_map/ppermute | solution.py:236
